TPU v7x, 64 devices: a 2x2x8 block of a 4x4x8 slice. The times are simulated.
64 devices in a mesh: member: 4 (over x, y), lat: 16 (over z, core).
Axes of the slice: x: 2, y: 2, z: 8, core: 2. Of those that a mesh axis runs over, the one named last changes fastest.
The devices are a block of a 4x4x8 slice.
Arguments:
- field: float32 [512, 256, 512], P('member', 'lat'), parts along dimension 0
- p_fwd: float32 [256, 256, 256], replicated
- p_inv: float32 [256, 256, 256], replicated
- w_mix: float32 [256, 128, 128, 2], replicated
Outputs:
- output: float32 [512, 256, 512], P('member', 'lat'), parts along dimension 0
There are 4 independent parts. A program takes and returns all parts, laid end to end along the dimension named above; an argument that names none is the same for every part.
All inputs are finite; a program needn't handle non-finite values.
Results may differ from a plain program's by a relative error of at most 0.0116587.
Values are sent between devices in bfloat16 or wider.
A program may use at most 768 MiB of HBM per device.

v0:
```python
import math
import jax
import jax.numpy as jnp
from jax import lax
from jax.sharding import PartitionSpec as P


def wave_tables(n_lon, groups, per_dev):
    wave_num = jnp.arange(per_dev, dtype=jnp.int32)[None, :] * groups + jnp.arange(groups, dtype=jnp.int32)[:, None]
    lon_idx = jnp.arange(n_lon, dtype=jnp.int32)
    phase_int = (wave_num[:, :, None] * lon_idx[None, None, :]) % n_lon
    phase_ang = phase_int.astype(jnp.float32) * (2.0 * math.pi / n_lon)
    fwd_tab = jnp.stack([jnp.cos(phase_ang), -jnp.sin(phase_ang)], axis=1)
    weight = jnp.where(wave_num == 0, 1.0, 2.0).astype(jnp.float32)[:, None, :, None]
    return fwd_tab, fwd_tab * weight


def mix_matrix(w_mix):
    w_re = w_mix[..., 0]
    w_im = w_mix[..., 1]
    from_re = jnp.stack([w_re, w_im], axis=2)
    from_im = jnp.stack([-w_im, w_re], axis=2)
    return jnp.stack([from_re, from_im], axis=1)


def solution(mesh):
    groups = mesh.shape["lat"]

    def local_layer(field_loc, p_fwd, p_inv, w_mix):
        n_chan, lat_loc, n_lon = field_loc.shape
        l_max = p_fwd.shape[0]
        n_lat = p_fwd.shape[2]
        per_dev = l_max // groups
        dev_index = lax.axis_index("lat")
        fwd_tab, inv_tab = wave_tables(n_lon, groups, per_dev)
        spec_loc = jnp.einsum("ctj,dqkj->ctdqk", field_loc, fwd_tab, preferred_element_type=jnp.float32).astype(jnp.bfloat16)
        spec_all = lax.all_to_all(spec_loc, "lat", split_axis=2, concat_axis=1)
        spec_all = spec_all.reshape(n_chan, n_lat, 2, per_dev)
        fwd_own = lax.dynamic_index_in_dim(p_fwd.reshape(per_dev, groups, l_max, n_lat), dev_index, axis=1, keepdims=False)
        inv_own = lax.dynamic_index_in_dim(p_inv.reshape(per_dev, groups, l_max, n_lat), dev_index, axis=1, keepdims=False)
        coef_own = jnp.einsum("klt,ctqk->klqc", fwd_own, spec_all, preferred_element_type=jnp.float32)
        mix_out = jnp.einsum("klpe,lpeqo->klqo", coef_own, mix_matrix(w_mix), preferred_element_type=jnp.float32)
        back_loc = jnp.einsum("klt,klqo->otqk", inv_own, mix_out, preferred_element_type=jnp.float32).astype(jnp.bfloat16)
        back_loc = back_loc.reshape(n_chan, groups, lat_loc, 2, per_dev)
        back_all = lax.all_to_all(back_loc, "lat", split_axis=1, concat_axis=2)
        wave_out = jnp.einsum("ctdqk,dqkj->ctj", back_all, inv_tab, preferred_element_type=jnp.float32)
        return field_loc + jax.nn.gelu(wave_out)

    return jax.shard_map(local_layer, mesh=mesh, in_specs=(P("member", "lat", None), P(), P(), P()), out_specs=P("member", "lat", None), check_vma=False)
```

profile of v0, /device:TPU:21, one launch (start us, length us, event | category | flops | bytes accessed | tf_op | source)
XLA Modules:
  0.0 190.0 jit_solution(7688536030492980350)
XLA Ops:
  0.0 2.1 %fusion.43 = (f32[16,1,16,512]{3,2,1,0:T(8,128)S(1)}, f32[16,1,16,512]{3,2,1,0:T(8,128)S(1)}) fusion(s32[16,16]{1,0:T(8,128)S(1)} %iota_add_fusion), kind=kLoop, calls=%fused_computation.44 | loop fusion | flops 1966080 | bytes 1049600 | tf_op jit(solution)/shard_map/cos | solution.py:13
  2.2 6.4 %convert_bitcast_fusion.1 = bf16[128,1,16,16,2,16]{0,5,2,4,1,3:T(8,128)(2,1)} fusion(f32[128,16,512,1,1]{2,1,0,4,3:T(8,128)} %bitcast.84, f32[16,1,16,512]{3,2,1,0:T(8,128)S(1)} %get-tuple-element.10, f32[16,1,16,512]{3,2,1,0:T(8,128)S(1)} %get-tuple-element.9), kind=kOutput, calls=%fused_computation.28 | convolution fusion | flops 1074790400 | bytes 7340032 | tf_op jit(solution)/shard_map/ctj,dqkj->ctdqk/dot_general | solution.py:36
  8.6 10.7 %all-to-all-start = ((bf16[128,1,16,16,2,16]{0,5,2,4,1,3:T(8,128)(2,1)}), bf16[128,1,16,16,2,16]{0,5,2,4,1,3:T(8,128)(2,1)S(1)}, u32[]{:S(2)}, u32[]{:S(2)}) async-start(bf16[128,1,16,16,2,16]{0,5,2,4,1,3:T(8,128)(2,1)} %convert_bitcast_fusion.1), calls=%async_computation | async-start | bytes 4194304 | tf_op jit(solution)/shard_map/all_to_all | solution.py:37
  19.3 37.6 %fusion.48 = (f32[256,128,128,1]{2,3,1,0:T(1,128)}, f32[256,128,128,1]{2,3,1,0:T(1,128)}) fusion(f32[256,128,128,2]{2,3,1,0:T(2,128)} %param.7), kind=kLoop, calls=%fused_computation.52 | loop fusion | bytes 67108864 | tf_op jit(solution)/shard_map/slice | solution.py:20
  56.9 9.5 %neg.20 = bf16[256,128,1,128]{3,1,2,0:T(8,128)(2,1)} negate(f32[256,128,1,128]{3,1,2,0:T(8,128)} %bitcast.79) | non-fusion elementwise | flops 4194304 | bytes 25165824 | tf_op jit(solution)/shard_map/neg | solution.py:22
  66.4 30.7 %maximum_bitcast_fusion = (bf16[256,1,128,2,128]{4,2,3,0,1:T(8,128)(2,1)}, bf16[256,1,128,2,128]{4,2,3,0,1:T(8,128)(2,1)}) fusion(f32[256,128,1,128]{3,1,2,0:T(8,128)} %bitcast.80, f32[256,128,1,128]{3,1,2,0:T(8,128)} %bitcast.81, bf16[256,128,1,128]{3,1,2,0:T(8,128)(2,1)} %neg.20), kind=kLoop, calls=%fused_computation.3 | loop fusion | flops 16777216 | bytes 75497472 | tf_op jit(solution)/shard_map/stack | solution.py:23
  97.1 0.0 all-to-all-done
  97.1 0.4 copy.23
  97.6 3.7 %fusion.19 = bf16[16,256,2,128,1]{1,3,2,0,4:T(8,128)(2,1)S(1)} fusion(f32[16,16,256,256]{3,2,1,0:T(8,128)} %bitcast.13, s32[]{:T(128)S(6)} %select_n.34, bf16[128,256,2,16]{0,3,2,1:T(8,128)(2,1)S(1)} %bitcast.82), kind=kOutput, calls=%fused_computation.23 | convolution fusion | flops 536870912 | bytes 6291460 | tf_op jit(solution)/shard_map/klt,ctqk->klqc/dot_general | solution.py:41
  101.2 3.1 %copy.37 = bf16[16,256,2,128,1]{3,0,1,4,2:T(8,128)(2,1)} copy(bf16[16,256,2,128,1]{1,3,2,0,4:T(8,128)(2,1)S(1)} %fusion.19) | data formatting | bytes 4194304 | tf_op jit(solution)/shard_map/klt,ctqk->klqc/transpose | solution.py:41
  104.3 12.7 %fusion.22 = bf16[16,256,2,128]{3,0,1,2:T(8,128)(2,1)S(1)} fusion(bf16[16,256,2,128,1]{3,0,1,4,2:T(8,128)(2,1)} %copy.37, bf16[256,1,128,2,128]{4,2,3,0,1:T(8,128)(2,1)} %get-tuple-element.8, bf16[256,1,128,2,128]{4,2,3,0,1:T(8,128)(2,1)} %get-tuple-element.7), kind=kOutput, calls=%fused_computation.24 | convolution fusion | flops 553648128 | bytes 37748736 | tf_op jit(solution)/shard_map/klpe,lpeqo->klqo/dot_general | solution.py:42
  117.1 3.5 %convert_bitcast_fusion = bf16[128,256,2,16]{1,0,2,3:T(8,128)(2,1)S(1)} fusion(f32[16,16,256,256]{3,2,1,0:T(8,128)} %bitcast.22, s32[]{:T(128)S(6)} %select_n.34, bf16[16,256,2,128]{3,0,1,2:T(8,128)(2,1)S(1)} %fusion.22), kind=kOutput, calls=%fused_computation.27 | convolution fusion | flops 536870912 | bytes 6291460 | tf_op jit(solution)/shard_map/klt,klqo->otqk/dot_general | solution.py:43
  120.5 3.1 %copy.29 = bf16[128,256,2,16]{0,3,2,1:T(8,128)(2,1)} copy(bf16[128,256,2,16]{1,0,2,3:T(8,128)(2,1)S(1)} %convert_bitcast_fusion) | data formatting | bytes 4194304 | tf_op jit(solution)/shard_map/convert_element_type | solution.py:43
  123.6 7.2 %all-to-all-start.1 = ((bf16[128,16,16,1,2,16]{0,5,4,2,3,1:T(8,128)(2,1)}), bf16[128,16,16,1,2,16]{0,5,4,2,3,1:T(8,128)(2,1)S(1)}, u32[]{:S(2)}, u32[]{:S(2)}) async-start(bf16[128,16,16,1,2,16]{0,5,4,2,3,1:T(8,128)(2,1)} %bitcast.83), calls=%async_computation.1 | async-start | bytes 4194304 | tf_op jit(solution)/shard_map/all_to_all | solution.py:45
  130.9 48.8 %all-to-all-done.1 = bf16[128,16,16,1,2,16]{0,5,4,2,3,1:T(8,128)(2,1)S(1)} async-done(((bf16[128,16,16,1,2,16]{0,5,4,2,3,1:T(8,128)(2,1)}), bf16[128,16,16,1,2,16]{0,5,4,2,3,1:T(8,128)(2,1)S(1)}, u32[]{:S(2)}, u32[]{:S(2)}) %all-to-all-start.1) | async-done | bytes 2097184 | tf_op jit(solution)/shard_map/all_to_all | solution.py:45
  179.6 5.9 %fusion.9 = f32[128,16,512]{2,0,1:T(8,128)S(1)} fusion(f32[128,16,512]{2,1,0:T(8,128)} %param.4, bf16[128,16,16,1,2,16]{0,5,4,2,3,1:T(8,128)(2,1)S(1)} %all-to-all-done.1, f32[16,1,16,512]{3,2,1,0:T(8,128)S(1)} %get-tuple-element.10, f32[16,1,16,512]{3,2,1,0:T(8,128)S(1)} %get-tuple-element.9, f32[16,16]{1,0:T(8,128)S(1)} %compare_select_fusion), kind=kOutput, calls=%fused_computation.13 | convolution fusion | flops 1083703296 | bytes 11535360 | tf_op jit(solution)/shard_map/ctdqk,dqkj->ctj/dot_general | solution.py:46
  185.6 4.4 %copy.32 = f32[128,16,512]{2,1,0:T(8,128)} copy(f32[128,16,512]{2,0,1:T(8,128)S(1)} %fusion.9) | data formatting | bytes 8388608 | tf_op jit(solution)/shard_map/add | solution.py:47
  (3 shorter events, 0.0 us)
Async XLA Ops:
  8.6 88.6 %all-to-all-start = ((bf16[128,1,16,16,2,16]{0,5,2,4,1,3:T(8,128)(2,1)}), bf16[128,1,16,16,2,16]{0,5,2,4,1,3:T(8,128)(2,1)S(1)}, u32[]{:S(2)}, u32[]{:S(2)}) async-start(bf16[128,1,16,16,2,16]{0,5,2,4,1,3:T(8,128)(2,1)} %convert_bitcast_fusion.1), calls=%async_computation | async-start | bytes 4194304 | tf_op jit(solution)/shard_map/all_to_all | solution.py:37
  123.6 56.0 %all-to-all-start.1 = ((bf16[128,16,16,1,2,16]{0,5,4,2,3,1:T(8,128)(2,1)}), bf16[128,16,16,1,2,16]{0,5,4,2,3,1:T(8,128)(2,1)S(1)}, u32[]{:S(2)}, u32[]{:S(2)}) async-start(bf16[128,16,16,1,2,16]{0,5,4,2,3,1:T(8,128)(2,1)} %bitcast.83), calls=%async_computation.1 | async-start | bytes 4194304 | tf_op jit(solution)/shard_map/all_to_all | solution.py:45
where the time goes:
time: 190 us
  waiting for transfers between devices  48.8 us (26%)
  local copies, waits for them, and re-layouts  48.6 us (26%)
  other arithmetic  42.4 us (22%)
  matrix products  32.3 us (17%)
  starting transfers between devices  18 us (9%)
    all_to_all x1, waiting for transfers between devices, local_layer(): back_all = lax.all_to_all(back_loc, 'lat', split_axis=1, concat_axis=2)  48.8 us
    slice x1, local copies, waits for them, and re-layouts, mix_matrix(): w_im = w_mix[..., 1]  37.6 us
    another operation x1, other arithmetic, mix_matrix(): return jnp.stack([from_re, from_im], axis=1)  30.7 us
    dot_general x1, matrix products, local_layer(): jnp.einsum('klpe,lpeqo->klqo', coef_own, mix_matrix(w_mix), preferred_ele...  12.7 us
    all_to_all x1, starting transfers between devices, local_layer(): spec_all = lax.all_to_all(spec_loc, 'lat', split_axis=2, concat_axis=1)  10.7 us
    neg x1, other arithmetic, mix_matrix(): from_im = jnp.stack([-w_im, w_re], axis=2)  9.5 us
    all_to_all x1, starting transfers between devices, local_layer(): back_all = lax.all_to_all(back_loc, 'lat', split_axis=1, concat_axis=2)  7.24 us
    dot_general x1, matrix products, local_layer(): jnp.einsum('ctj,dqkj->ctdqk', field_loc, fwd_tab, preferred_element_type=...  6.43 us
  transfers between devices with their start and end apart: 2, of which 1 were waited for; matrix products, arithmetic and copies ran while one was open for 41% of the time, Pallas kernels for 0%

commit v1 on v0

v1 whole, which is shorter than its diff:
```python
import functools
import math

import jax
import jax.numpy as jnp
import numpy as np
from jax import lax
from jax.experimental import pallas as pl
from jax.experimental.pallas import tpu as pltpu
from jax.sharding import PartitionSpec as P

MESH = pl.DeviceIdType.MESH
F32 = jnp.float32
BF16 = jnp.bfloat16
LANES = 128
N_CHUNK = 4


def wave_tables(n_lon, groups, per_dev, n_chunk):
    piece = per_dev // n_chunk
    chunk, dev, part, k = np.meshgrid(np.arange(n_chunk), np.arange(groups), np.arange(2), np.arange(piece), indexing="ij")
    wave = ((chunk * piece + k) * groups + dev).reshape(-1, 1)
    part = part.reshape(-1, 1)
    angle = ((wave * np.arange(n_lon)[None, :]) % n_lon) * (2.0 * math.pi / n_lon)
    fwd = np.where(part == 0, np.cos(angle), -np.sin(angle)).astype(np.float32)
    inv = fwd * np.where(wave == 0, 1.0, 2.0).astype(np.float32)
    return jnp.asarray(fwd, BF16), jnp.asarray(inv, BF16)


def dot(a, b, dims):
    return lax.dot_general(a, b, (dims, ((), ())), preferred_element_type=F32)


def layer_kernel(dims, f_hbm, pw_hbm, pi_hbm, w_hbm, tf_hbm, ti_hbm, o_hbm,
                 f_v, h_v, w_v, stage, pw_v, pi_v, f_send, f_recv, g_send, g_recv, wide, coef, tf_v, ti_v,
                 in_sem, f_sem, pw_sem, pi_sem, w_sem, own_sem, fs_sem, fr_sem, gs_sem, gr_sem):
    groups, n_chan, lat_loc, n_lon, l_max, n_lat, n_chunk = dims
    per_dev = l_max // groups
    piece = per_dev // n_chunk
    rows = 2 * piece
    block = lat_loc * rows
    l_step = l_max // n_chunk
    member, me = lax.axis_index("member"), lax.axis_index("lat")
    n_z = groups // 2
    z, core = me // 2, lax.rem(me, 2)

    def peer(i):
        step = i // 2
        dist = n_z // 2 - (step + 1) // 2
        dz = jnp.where(lax.rem(step, 2) == 1, dist, -dist)
        far = lax.rem(z + dz + n_z, n_z) * 2 + lax.rem(i, 2)
        return jnp.where(i == groups - 2, z * 2 + 1 - core, far)

    barrier = pltpu.get_barrier_semaphore()

    def greet(i, _):
        pl.semaphore_signal(barrier, inc=1, device_id=(member, peer(i)), device_id_type=MESH)
        return 0

    lax.fori_loop(0, groups - 1, greet, 0)

    n_col = n_lon // LANES

    def f_in(x):
        return pltpu.make_async_copy(f_hbm.at[:, pl.ds(x * LANES, LANES)], f_v.at[x], f_sem.at[x])

    def f_out(x):
        return pltpu.make_async_copy(f_v.at[x], o_hbm.at[:, pl.ds(x * LANES, LANES)], f_sem.at[x])

    tf_in = pltpu.make_async_copy(tf_hbm, tf_v, in_sem.at[0])
    ti_in = pltpu.make_async_copy(ti_hbm, ti_v, in_sem.at[1])
    tf_in.start()
    for x in range(n_col):
        f_in(x).start()

    def table_copy(src, dst, sem, k):
        low = k * groups
        return pltpu.make_async_copy(src.at[k * groups + me, pl.ds(low, l_max - low), :], dst.at[k, pl.ds(low, l_max - low), :], sem.at[k])

    n_slot = stage.shape[0]
    w_blk = stage.shape[1] // (2 * n_chan)
    n_blk = l_max // w_blk
    blk_rows = stage.shape[1]

    def w_copy(b, slot):
        return pltpu.make_async_copy(w_hbm.at[pl.ds((n_blk - 1 - b) * blk_rows, blk_rows), :], stage.at[slot], w_sem.at[slot])

    for s in range(n_slot):
        w_copy(s, s).start()
    for k in reversed(range(per_dev)):
        table_copy(pw_hbm, pw_v, pw_sem, k).start()
        low, first = k * groups, (k // piece) * l_step
        if low > first:
            pw_v[k, first:low, :] = jnp.zeros((low - first, n_lat), F32)
            pi_v[k, first:low, :] = jnp.zeros((low - first, n_lat), F32)
        table_copy(pi_hbm, pi_v, pi_sem, k).start()
    ti_in.start()

    tf_in.wait()
    for x in range(n_col):
        f_in(x).wait()

    def dft(u, _):
        out = []
        for half in range(2):
            here = pl.ds(2 * u + half, n_chan, stride=lat_loc)
            f_t = jnp.concatenate([f_v[x, here, :] for x in range(n_col)], axis=1).astype(BF16)
            r = dot(tf_v[...], f_t, ((1,), (1,)))
            out.append(r.reshape(n_chunk * groups, rows, n_chan))
        f_send[:, pl.ds(pl.multiple_of(u * 2 * rows, 2 * rows), 2 * rows), :] = jnp.concatenate(out, axis=1).astype(BF16)
        return 0

    lax.fori_loop(0, lat_loc // 2, dft, 0)
    pl.semaphore_wait(barrier, groups - 1)

    def fwd_copy(j, to, slot):
        return pltpu.make_async_remote_copy(
            src_ref=f_send.at[j * groups + to], dst_ref=f_recv.at[j * groups + slot], send_sem=fs_sem.at[j, to],
            recv_sem=fr_sem.at[j, slot], device_id=(member, to), device_id_type=MESH)

    def back_copy(j, to, slot):
        return pltpu.make_async_remote_copy(
            src_ref=g_send.at[j * groups + to], dst_ref=g_recv.at[j * groups + slot], send_sem=gs_sem.at[j, to],
            recv_sem=gr_sem.at[j, slot], device_id=(member, to), device_id_type=MESH)

    def send_all(copy, src, dst, j, own):
        pltpu.make_async_copy(src.at[j * groups + me], dst.at[j * groups + me], own_sem.at[own]).start()

        def go(i, _):
            copy(j, peer(i), me).start()
            return 0

        lax.fori_loop(0, groups - 1, go, 0)

    def recv_all(copy, src, dst, j, own):
        pltpu.make_async_copy(src.at[j * groups + me], dst.at[j * groups + me], own_sem.at[own]).wait()

        def got(i, _):
            s = lax.rem(me + i, groups)
            copy(j, s, s).wait_recv()
            return 0

        lax.fori_loop(1, groups, got, 0)

    def sent_all(copy, j):
        def done(i, _):
            s = lax.rem(me + i, groups)
            copy(j, s, s).wait_send()
            return 0

        lax.fori_loop(1, groups, done, 0)

    order = list(reversed(range(n_chunk)))
    for j in order:
        send_all(fwd_copy, f_send, f_recv, j, j)

    sign = jnp.where(lax.broadcasted_iota(jnp.int32, (rows, n_chan), 0) < piece, -1.0, 1.0).astype(F32)

    def load_w(b, _):
        slot = lax.rem(b, n_slot)
        w_copy(b, slot).wait()
        half = blk_rows // 2
        re = stage[slot, pl.ds(0, half, stride=2), :]
        im = stage[slot, pl.ds(1, half, stride=2), :]
        at = pl.ds(pl.multiple_of((n_blk - 1 - b) * half, half), half)
        w_v[at, :n_chan] = re.astype(BF16)
        w_v[at, n_chan:] = im.astype(BF16)

        @pl.when(b + n_slot < n_blk)
        def _():
            w_copy(b + n_slot, slot).start()

        return 0

    blk_chunk = n_blk // n_chunk
    n_row = n_lat * rows
    for at, j in enumerate(order):
        lax.fori_loop(at * blk_chunk, (at + 1) * blk_chunk, load_w, 0)
        recv_all(fwd_copy, f_send, f_recv, j, j)
        low = j * l_step
        n_l = l_max - low

        def widen(s, _):
            wide[pl.ds(pl.multiple_of(s * block, block), block), :] = f_recv[j * groups + s].astype(F32)
            return 0

        lax.fori_loop(0, groups, widen, 0)
        for i in range(piece):
            k = j * piece + i
            table_copy(pw_hbm, pw_v, pw_sem, k).wait()
            re = wide[pl.ds(i, n_lat, stride=rows), :]
            im = wide[pl.ds(piece + i, n_lat, stride=rows), :]
            spec = jnp.concatenate([re, im], axis=1).astype(BF16)
            a = dot(pw_v[k, low:, :].astype(BF16), spec, ((1,), (0,)))
            coef[pl.ds(low * rows + i, n_l, stride=rows), :] = a[:, :n_chan]
            coef[pl.ds(low * rows + piece + i, n_l, stride=rows), :] = a[:, n_chan:]

        def mix(v, _):
            for e in range(8):
                deg = v * 8 + e
                here = pl.ds(pl.multiple_of(deg * rows, rows), rows)
                w_l = w_v[pl.ds(pl.multiple_of(deg * n_chan, n_chan), n_chan), :]
                r = dot(coef[here, :].astype(BF16), w_l, ((1,), (0,)))
                coef[here, :] = r[:, :n_chan] + sign * pltpu.roll(r[:, n_chan:], piece, 0)
            return 0

        lax.fori_loop(low // 8, l_max // 8, mix, 0)
        for i in range(piece):
            k = j * piece + i
            table_copy(pi_hbm, pi_v, pi_sem, k).wait()
            re = coef[pl.ds(low * rows + i, n_l, stride=rows), :]
            im = coef[pl.ds(low * rows + piece + i, n_l, stride=rows), :]
            b = jnp.concatenate([re, im], axis=1).astype(BF16)
            g = dot(pi_v[k, low:, :].astype(BF16), b, ((0,), (0,)))
            wide[pl.ds(i, n_lat, stride=rows), :] = g[:, :n_chan]
            wide[pl.ds(piece + i, n_lat, stride=rows), :] = g[:, n_chan:]

        def narrow(s, _):
            g_send[j * groups + s] = wide[pl.ds(pl.multiple_of(s * block, block), block), :].astype(BF16)
            return 0

        lax.fori_loop(0, groups, narrow, 0)
        send_all(back_copy, g_send, g_recv, j, n_chunk + j)

    ti_in.wait()
    for at, j in enumerate(order):
        recv_all(back_copy, g_send, g_recv, j, n_chunk + j)
        last = at == n_chunk - 1

        def inverse(u, _):
            pair = g_recv[j * groups:(j + 1) * groups, pl.ds(pl.multiple_of(u * 2 * rows, 2 * rows), 2 * rows), :].astype(F32)
            for half in range(2):
                t = 2 * u + half
                g_t = pair[:, half * rows:(half + 1) * rows, :].reshape(groups * rows, n_chan)
                h = dot(g_t.T.astype(BF16), ti_v[j * groups * rows:(j + 1) * groups * rows, :], ((1,), (0,)))
                if at > 0:
                    h = h + h_v[t]
                if last:
                    here = pl.ds(t, n_chan, stride=lat_loc)
                    g = jax.nn.gelu(h)
                    for x in range(n_col):
                        f_v[x, here, :] = f_v[x, here, :] + g[:, x * LANES:(x + 1) * LANES]
                else:
                    h_v[t] = h
            return 0

        lax.fori_loop(0, lat_loc // 2, inverse, 0)
    for x in range(n_col):
        f_out(x).start()
    for j in order:
        sent_all(fwd_copy, j)
        sent_all(back_copy, j)
    for x in range(n_col):
        f_out(x).wait()


def solution(mesh):
    groups = mesh.shape["lat"]

    def local_layer(field_loc, p_fwd, p_inv, w_mix):
        n_chan, lat_loc, n_lon = field_loc.shape
        l_max, _, n_lat = p_fwd.shape
        per_dev = l_max // groups
        rows = 2 * per_dev // N_CHUNK
        block = lat_loc * rows
        fwd_tab, inv_tab = wave_tables(n_lon, groups, per_dev, N_CHUNK)
        w_rows = w_mix.transpose(0, 1, 3, 2).reshape(l_max * n_chan * 2, n_chan)
        hbm = pl.BlockSpec(memory_space=pltpu.HBM)
        exchange = pltpu.VMEM((N_CHUNK * groups, block, n_chan), BF16)
        dma = pltpu.SemaphoreType.DMA
        out = pl.pallas_call(
            functools.partial(layer_kernel, (groups, n_chan, lat_loc, n_lon, l_max, n_lat, N_CHUNK)),
            out_shape=jax.ShapeDtypeStruct((n_chan * lat_loc, n_lon), F32),
            in_specs=[hbm] * 6,
            out_specs=hbm,
            scratch_shapes=[
                pltpu.VMEM((n_lon // LANES, n_chan * lat_loc, LANES), F32),
                pltpu.VMEM((lat_loc, n_chan, n_lon), F32),
                pltpu.VMEM((l_max * n_chan, 2 * n_chan), BF16),
                pltpu.VMEM((4, 8 * n_chan * 2, n_chan), F32),
                pltpu.VMEM((per_dev, l_max, n_lat), F32),
                pltpu.VMEM((per_dev, l_max, n_lat), F32),
                exchange, exchange, exchange, exchange,
                pltpu.VMEM((n_lat * rows, n_chan), F32),
                pltpu.VMEM((l_max * rows, n_chan), F32),
                pltpu.VMEM(fwd_tab.shape, BF16),
                pltpu.VMEM(inv_tab.shape, BF16),
                dma((2,)), dma((n_lon // LANES,)), dma((per_dev,)), dma((per_dev,)), dma((4,)), dma((2 * N_CHUNK,)),
                dma((N_CHUNK, groups)), dma((N_CHUNK, groups)), dma((N_CHUNK, groups)), dma((N_CHUNK, groups)),
            ],
            compiler_params=pltpu.CompilerParams(collective_id=0, has_side_effects=True, vmem_limit_bytes=62 * 2**20),
            name="spectral_layer",
        )(field_loc.reshape(n_chan * lat_loc, n_lon), p_fwd, p_inv, w_rows, fwd_tab, inv_tab)
        return out.reshape(field_loc.shape)

    return jax.shard_map(local_layer, mesh=mesh, in_specs=(P("member", "lat", None), P(), P(), P()), out_specs=P("member", "lat", None), check_vma=False)
```

time: 190 us -> 123 us (0.65)
  Pallas kernels: 0 us -> 118 us
  waiting for transfers between devices: 48.8 us -> 0 us
  local copies, waits for them, and re-layouts: 48.6 us -> 5.04 us
  other arithmetic: 42.4 us -> 0 us
  matrix products: 32.3 us -> 0 us
  starting transfers between devices: 18 us -> 0 us
    pallas_call x0 -> x1, Pallas kernels: none -> 118 us  [local_layer(): pl.pallas_call(functools.partial(layer_kernel, (groups, n_chan, lat_loc,...]
    all_to_all x2 -> x0, waiting for transfers between devices: 48.8 us -> none  [the longest x1 48.8 us: local_layer(): back_all = lax.all_to_all(back_loc, 'lat', split_axis=1, concat_axis=2)]
    slice x1 -> x0, local copies, waits for them, and re-layouts: 37.6 us -> none  [mix_matrix(): w_im = w_mix[..., 1]]
    dot_general x5 -> x0, matrix products: 32.3 us -> none  [the longest x1 12.7 us: local_layer(): jnp.einsum('klpe,lpeqo->klqo', coef_own, mix_matrix(w_mix), preferred_ele...]
    another operation x1 -> x0, other arithmetic: 30.7 us -> none  [mix_matrix(): return jnp.stack([from_re, from_im], axis=1)]
    all_to_all x2 -> x0, starting transfers between devices: 18 us -> none  [the longest x1 10.7 us: local_layer(): spec_all = lax.all_to_all(spec_loc, 'lat', split_axis=2, concat_axis=1)]
    neg x1 -> x0, other arithmetic: 9.5 us -> none  [mix_matrix(): from_im = jnp.stack([-w_im, w_re], axis=2)]
    unnamed x0 -> x1, local copies, waits for them, and re-layouts: none -> 5.04 us
  transfers between devices with their start and end apart: 2 -> 0, of which waited for: 1 -> 0; matrix products, arithmetic and copies ran while one was open for 41% -> 0% of each run, Pallas kernels for 0% -> 0%
where the time goes in v1:
time: 123 us
  Pallas kernels  118 us (96%)
  local copies, waits for them, and re-layouts  5.04 us (4%)
    pallas_call x1, Pallas kernels, local_layer(): pl.pallas_call(functools.partial(layer_kernel, (groups, n_chan, lat_loc,...  118 us
    unnamed x1, local copies, waits for them, and re-layouts  5.04 us

profile of v1, /device:TPU:21, one launch (start us, length us, event | category | flops | bytes accessed | tf_op | source)
XLA Modules:
  0.0 122.8 jit_solution(453463781760634438)
XLA Ops:
  0.0 117.7 %spectral_layer.1 = f32[2048,512]{1,0:T(8,128)} custom-call(f32[2048,512]{1,0:T(8,128)} %bitcast.7, f32[256,256,256]{2,1,0:T(8,128)} %pw_hbm.1, f32[256,256,256]{2,1,0:T(8,128)} %pi_hbm.1, f32[65536,128]{1,0:T(8,128)} %bitcast.5, bf16[512,512]{1,0:T(8,128)(2,1)} %constant.4.clone.tf_hbm, bf16[512,512]{1,0:T(8,128)(2,1)} %constant.5.clone.ti_hbm), custom_call_target="tpu_custom_call" | custom-call | tf_op jit(solution)/shard_map/spectral_layer/pallas_call | solution.py:271
  117.7 5.0 %copy.8 = f32[128,16,512]{2,1,0:T(8,128)} copy(f32[128,16,512]{2,1,0:T(8,128)} %bitcast.6) | data formatting | bytes 8388608

commit v2 on v1

--- a/solution.py
+++ b/solution.py
@@ -31,9 +31,11 @@
     return lax.dot_general(a, b, (dims, ((), ())), preferred_element_type=F32)
 
 
-def layer_kernel(dims, f_hbm, pw_hbm, pi_hbm, w_hbm, tf_hbm, ti_hbm, o_hbm,
-                 f_v, h_v, w_v, stage, pw_v, pi_v, f_send, f_recv, g_send, g_recv, wide, coef, tf_v, ti_v,
-                 in_sem, f_sem, pw_sem, pi_sem, w_sem, own_sem, fs_sem, fr_sem, gs_sem, gr_sem):
+def layer_kernel(dims, f_hbm, pw_hbm, pi_hbm, w_hbm, tf_hbm, ti_hbm, *refs):
+    n_out = dims[3] // LANES
+    o_v, refs = refs[:n_out], refs[n_out:]
+    (f_v, f_b, h_v, w_v, stage, pw_v, pi_v, f_send, f_recv, g_send, g_recv, wide, coef, tf_v, ti_v,
+                 in_sem, f_sem, pw_sem, pi_sem, w_sem, own_sem, fs_sem, fr_sem, gs_sem, gr_sem) = refs
     groups, n_chan, lat_loc, n_lon, l_max, n_lat, n_chunk = dims
     per_dev = l_max // groups
     piece = per_dev // n_chunk
@@ -61,17 +63,18 @@
 
     n_col = n_lon // LANES
 
-    def f_in(x):
-        return pltpu.make_async_copy(f_hbm.at[:, pl.ds(x * LANES, LANES)], f_v.at[x], f_sem.at[x])
-
-    def f_out(x):
-        return pltpu.make_async_copy(f_v.at[x], o_hbm.at[:, pl.ds(x * LANES, LANES)], f_sem.at[x])
+    half = lat_loc // 2
+
+    def f_in(h, x):
+        part = pl.ds(h * half, half)
+        return pltpu.make_async_copy(f_hbm.at[:, part, pl.ds(x * LANES, LANES)], f_v.at[x, :, part, :], f_sem.at[h, x])
 
     tf_in = pltpu.make_async_copy(tf_hbm, tf_v, in_sem.at[0])
     ti_in = pltpu.make_async_copy(ti_hbm, ti_v, in_sem.at[1])
     tf_in.start()
-    for x in range(n_col):
-        f_in(x).start()
+    for h in range(2):
+        for x in range(n_col):
+            f_in(h, x).start()
 
     def table_copy(src, dst, sem, k):
         low = k * groups
@@ -85,32 +88,43 @@
     def w_copy(b, slot):
         return pltpu.make_async_copy(w_hbm.at[pl.ds((n_blk - 1 - b) * blk_rows, blk_rows), :], stage.at[slot], w_sem.at[slot])
 
-    for s in range(n_slot):
-        w_copy(s, s).start()
-    for k in reversed(range(per_dev)):
-        table_copy(pw_hbm, pw_v, pw_sem, k).start()
-        low, first = k * groups, (k // piece) * l_step
-        if low > first:
-            pw_v[k, first:low, :] = jnp.zeros((low - first, n_lat), F32)
-            pi_v[k, first:low, :] = jnp.zeros((low - first, n_lat), F32)
-        table_copy(pi_hbm, pi_v, pi_sem, k).start()
-    ti_in.start()
+    def start_loads():
+        for s in range(n_slot):
+            w_copy(s, s).start()
+        for k in reversed(range(per_dev)):
+            table_copy(pw_hbm, pw_v, pw_sem, k).start()
+            low, first = k * groups, (k // piece) * l_step
+            if low > first:
+                pw_v[k, first:low, :] = jnp.zeros((low - first, n_lat), F32)
+                pi_v[k, first:low, :] = jnp.zeros((low - first, n_lat), F32)
+            table_copy(pi_hbm, pi_v, pi_sem, k).start()
+        ti_in.start()
 
     tf_in.wait()
-    for x in range(n_col):
-        f_in(x).wait()
-
-    def dft(u, _):
-        out = []
-        for half in range(2):
-            here = pl.ds(2 * u + half, n_chan, stride=lat_loc)
-            f_t = jnp.concatenate([f_v[x, here, :] for x in range(n_col)], axis=1).astype(BF16)
-            r = dot(tf_v[...], f_t, ((1,), (1,)))
-            out.append(r.reshape(n_chunk * groups, rows, n_chan))
-        f_send[:, pl.ds(pl.multiple_of(u * 2 * rows, 2 * rows), 2 * rows), :] = jnp.concatenate(out, axis=1).astype(BF16)
+    f_rows = f_v.reshape(n_col, n_chan * lat_loc, LANES)
+
+    def dft_out(j, u, f_pair):
+        r = dot(tf_v[j * groups * rows:(j + 1) * groups * rows, :], f_pair, ((1,), (1,)))
+        both = [r[:, e * n_chan:(e + 1) * n_chan].reshape(groups, rows, n_chan) for e in range(2)]
+        at = pl.ds(pl.multiple_of(u * 2 * rows, 2 * rows), 2 * rows)
+        f_send[j * groups:(j + 1) * groups, at, :] = jnp.concatenate(both, axis=1).astype(BF16)
+
+    def dft_first(u, _):
+        pair = []
+        for e in range(2):
+            here = pl.ds(2 * u + e, n_chan, stride=lat_loc)
+            pair.append(jnp.concatenate([f_rows[x, here, :] for x in range(n_col)], axis=1))
+        f_pair = jnp.concatenate(pair, axis=0).astype(BF16)
+        f_b[u] = f_pair
+        dft_out(n_chunk - 1, u, f_pair)
         return 0
 
-    lax.fori_loop(0, lat_loc // 2, dft, 0)
+    for h in range(2):
+        for x in range(n_col):
+            f_in(h, x).wait()
+        if h == 1:
+            start_loads()
+        lax.fori_loop(h * half // 2, (h + 1) * half // 2, dft_first, 0)
     pl.semaphore_wait(barrier, groups - 1)
 
     def fwd_copy(j, to, slot):
@@ -118,23 +132,25 @@
             src_ref=f_send.at[j * groups + to], dst_ref=f_recv.at[j * groups + slot], send_sem=fs_sem.at[j, to],
             recv_sem=fr_sem.at[j, slot], device_id=(member, to), device_id_type=MESH)
 
-    def back_copy(j, to, slot):
+    def back_copy(p, to, slot):
+        j, part = (p, pl.ds(0, block)) if p else (0, pl.ds(0, block // 2))
+        if p == n_chunk:
+            j, part = 0, pl.ds(block // 2, block // 2)
         return pltpu.make_async_remote_copy(
-            src_ref=g_send.at[j * groups + to], dst_ref=g_recv.at[j * groups + slot], send_sem=gs_sem.at[j, to],
-            recv_sem=gr_sem.at[j, slot], device_id=(member, to), device_id_type=MESH)
-
-    def send_all(copy, src, dst, j, own):
-        pltpu.make_async_copy(src.at[j * groups + me], dst.at[j * groups + me], own_sem.at[own]).start()
-
+            src_ref=g_send.at[j * groups + to, part], dst_ref=g_recv.at[j * groups + slot, part], send_sem=gs_sem.at[p, to],
+            recv_sem=gr_sem.at[p, slot], device_id=(member, to), device_id_type=MESH)
+
+    def own_copy(src, dst, j, own):
+        return pltpu.make_async_copy(src.at[j * groups + me], dst.at[j * groups + me], own_sem.at[own])
+
+    def send_all(copy, j):
         def go(i, _):
             copy(j, peer(i), me).start()
             return 0
 
         lax.fori_loop(0, groups - 1, go, 0)
 
-    def recv_all(copy, src, dst, j, own):
-        pltpu.make_async_copy(src.at[j * groups + me], dst.at[j * groups + me], own_sem.at[own]).wait()
-
+    def recv_all(copy, j):
         def got(i, _):
             s = lax.rem(me + i, groups)
             copy(j, s, s).wait_recv()
@@ -152,7 +168,10 @@
 
     order = list(reversed(range(n_chunk)))
     for j in order:
-        send_all(fwd_copy, f_send, f_recv, j, j)
+        if j < n_chunk - 1:
+            lax.fori_loop(0, lat_loc // 2, lambda u, _, j=j: dft_out(j, u, f_b[u]) or 0, 0)
+        own_copy(f_send, f_recv, j, j).start()
+        send_all(fwd_copy, j)
 
     sign = jnp.where(lax.broadcasted_iota(jnp.int32, (rows, n_chan), 0) < piece, -1.0, 1.0).astype(F32)
 
@@ -176,7 +195,8 @@
     n_row = n_lat * rows
     for at, j in enumerate(order):
         lax.fori_loop(at * blk_chunk, (at + 1) * blk_chunk, load_w, 0)
-        recv_all(fwd_copy, f_send, f_recv, j, j)
+        own_copy(f_send, f_recv, j, j).wait()
+        recv_all(fwd_copy, j)
         low = j * l_step
         n_l = l_max - low
 
@@ -220,11 +240,15 @@
             return 0
 
         lax.fori_loop(0, groups, narrow, 0)
-        send_all(back_copy, g_send, g_recv, j, n_chunk + j)
+        own_copy(g_send, g_recv, j, n_chunk + j).start()
+        send_all(back_copy, j)
+        if j == 0:
+            send_all(back_copy, n_chunk)
 
     ti_in.wait()
     for at, j in enumerate(order):
-        recv_all(back_copy, g_send, g_recv, j, n_chunk + j)
+        own_copy(g_send, g_recv, j, n_chunk + j).wait()
+        recv_all(back_copy, j)
         last = at == n_chunk - 1
 
         def inverse(u, _):
@@ -239,19 +263,21 @@
                     here = pl.ds(t, n_chan, stride=lat_loc)
                     g = jax.nn.gelu(h)
                     for x in range(n_col):
-                        f_v[x, here, :] = f_v[x, here, :] + g[:, x * LANES:(x + 1) * LANES]
+                        o_v[x][here, :] = f_rows[x, here, :] + g[:, x * LANES:(x + 1) * LANES]
                 else:
                     h_v[t] = h
             return 0
 
-        lax.fori_loop(0, lat_loc // 2, inverse, 0)
-    for x in range(n_col):
-        f_out(x).start()
+        if last:
+            lax.fori_loop(0, lat_loc // 4, inverse, 0)
+            recv_all(back_copy, n_chunk)
+            lax.fori_loop(lat_loc // 4, lat_loc // 2, inverse, 0)
+        else:
+            lax.fori_loop(0, lat_loc // 2, inverse, 0)
     for j in order:
         sent_all(fwd_copy, j)
         sent_all(back_copy, j)
-    for x in range(n_col):
-        f_out(x).wait()
+    sent_all(back_copy, n_chunk)
 
 
 def solution(mesh):
@@ -270,11 +296,12 @@
         dma = pltpu.SemaphoreType.DMA
         out = pl.pallas_call(
             functools.partial(layer_kernel, (groups, n_chan, lat_loc, n_lon, l_max, n_lat, N_CHUNK)),
-            out_shape=jax.ShapeDtypeStruct((n_chan * lat_loc, n_lon), F32),
+            out_shape=[pltpu.VMEM((n_chan * lat_loc, LANES), F32)] * (n_lon // LANES),
             in_specs=[hbm] * 6,
-            out_specs=hbm,
+            out_specs=[pl.BlockSpec(memory_space=pltpu.VMEM)] * (n_lon // LANES),
             scratch_shapes=[
-                pltpu.VMEM((n_lon // LANES, n_chan * lat_loc, LANES), F32),
+                pltpu.VMEM((n_lon // LANES, n_chan, lat_loc, LANES), F32),
+                pltpu.VMEM((lat_loc // 2, 2 * n_chan, n_lon), BF16),
                 pltpu.VMEM((lat_loc, n_chan, n_lon), F32),
                 pltpu.VMEM((l_max * n_chan, 2 * n_chan), BF16),
                 pltpu.VMEM((4, 8 * n_chan * 2, n_chan), F32),
@@ -285,12 +312,12 @@
                 pltpu.VMEM((l_max * rows, n_chan), F32),
                 pltpu.VMEM(fwd_tab.shape, BF16),
                 pltpu.VMEM(inv_tab.shape, BF16),
-                dma((2,)), dma((n_lon // LANES,)), dma((per_dev,)), dma((per_dev,)), dma((4,)), dma((2 * N_CHUNK,)),
-                dma((N_CHUNK, groups)), dma((N_CHUNK, groups)), dma((N_CHUNK, groups)), dma((N_CHUNK, groups)),
+                dma((2,)), dma((2, n_lon // LANES)), dma((per_dev,)), dma((per_dev,)), dma((4,)), dma((2 * N_CHUNK,)),
+                dma((N_CHUNK, groups)), dma((N_CHUNK, groups)), dma((N_CHUNK + 1, groups)), dma((N_CHUNK + 1, groups)),
             ],
-            compiler_params=pltpu.CompilerParams(collective_id=0, has_side_effects=True, vmem_limit_bytes=62 * 2**20),
+            compiler_params=pltpu.CompilerParams(collective_id=0, has_side_effects=True, vmem_limit_bytes=54 * 2**20),
             name="spectral_layer",
-        )(field_loc.reshape(n_chan * lat_loc, n_lon), p_fwd, p_inv, w_rows, fwd_tab, inv_tab)
-        return out.reshape(field_loc.shape)
+        )(field_loc, p_fwd, p_inv, w_rows, fwd_tab, inv_tab)
+        return jnp.concatenate([part.reshape(n_chan, lat_loc, LANES) for part in out], axis=2)
 
     return jax.shard_map(local_layer, mesh=mesh, in_specs=(P("member", "lat", None), P(), P(), P()), out_specs=P("member", "lat", None), check_vma=False)

time: 123 us -> 113 us (0.919)
  Pallas kernels: 118 us -> 110 us
  local copies, waits for them, and re-layouts: 5.04 us -> 0 us
  other arithmetic: 0 us -> 2.29 us
    pallas_call x1, Pallas kernels: 118 us -> 110 us  [local_layer(): pl.pallas_call(functools.partial(layer_kernel, (groups, n_chan, lat_loc,...]
    unnamed x1 -> x0, local copies, waits for them, and re-layouts: 5.04 us -> none
    concatenate x0 -> x1, other arithmetic: none -> 2.29 us  [local_layer(): jnp.concatenate([part.reshape(n_chan, lat_loc, LANES) for part in out], a...]
where the time goes in v2:
time: 113 us; the launch traced here: 112 us
  Pallas kernels  110 us (97%)
  other arithmetic  2.29 us (2%)
    pallas_call x1, Pallas kernels, local_layer(): pl.pallas_call(functools.partial(layer_kernel, (groups, n_chan, lat_loc,...  110 us
    concatenate x1, other arithmetic, local_layer(): jnp.concatenate([part.reshape(n_chan, lat_loc, LANES) for part in out], a...  2.29 us

profile of v2, /device:TPU:21, one launch (start us, length us, event | category | flops | bytes accessed | tf_op | source)
XLA Modules:
  0.0 112.0 jit_solution(1048248231921104909)
XLA Ops:
  0.0 109.7 %spectral_layer.1 = (f32[2048,128]{1,0:T(8,128)S(1)}, f32[2048,128]{1,0:T(8,128)S(1)}, f32[2048,128]{1,0:T(8,128)S(1)}, f32[2048,128]{1,0:T(8,128)S(1)}) custom-call(f32[128,16,512]{2,1,0:T(8,128)} %f_hbm.1, f32[256,256,256]{2,1,0:T(8,128)} %pw_hbm.1, f32[256,256,256]{2,1,0:T(8,128)} %pi_hbm.1, f32[65536,128]{1,0:T(8,128)} %bitcast.11, ...), custom_call_target="tpu_custom_call" | custom-call | tf_op jit(solution)/shard_map/spectral_layer/pallas_call | solution.py:297
  109.7 2.3 %pad_maximum_fusion = f32[128,16,512]{2,1,0:T(8,128)} fusion(f32[128,16,128]{2,1,0:T(8,128)S(1)} %bitcast.10, f32[128,16,128]{2,1,0:T(8,128)S(1)} %bitcast.9, f32[128,16,128]{2,1,0:T(8,128)S(1)} %bitcast.8, f32[128,16,128]{2,1,0:T(8,128)S(1)} %bitcast.7), kind=kLoop, calls=%fused_computation | loop fusion | flops 3145728 | bytes 8388608 | tf_op jit(solution)/shard_map/concatenate | solution.py:321

commit v3 on v2

--- a/solution.py
+++ b/solution.py
@@ -34,14 +34,18 @@
 def layer_kernel(dims, f_hbm, pw_hbm, pi_hbm, w_hbm, tf_hbm, ti_hbm, *refs):
     n_out = dims[3] // LANES
     o_v, refs = refs[:n_out], refs[n_out:]
-    (f_v, f_b, h_v, w_v, stage, pw_v, pi_v, f_send, f_recv, g_send, g_recv, wide, coef, tf_v, ti_v,
-                 in_sem, f_sem, pw_sem, pi_sem, w_sem, own_sem, fs_sem, fr_sem, gs_sem, gr_sem) = refs
+    (f_v, f_b, h_v, w_v, stage, pw_v, pi_v, f_send, f_recv, g_send, g_recv, wide, coef, b_all, pi_loc, tf_v, ti_v,
+                 in_sem, f_sem, pw_sem, pi_sem, w_sem, own_sem, fs_sem, fr_sem, gs_sem, gr_sem, hop_s, hop_r, sib_s, sib_r) = refs
     groups, n_chan, lat_loc, n_lon, l_max, n_lat, n_chunk = dims
     per_dev = l_max // groups
     piece = per_dev // n_chunk
     rows = 2 * piece
     block = lat_loc * rows
     l_step = l_max // n_chunk
+    top = n_chunk - 1
+    heights = [l_max - (top * piece + i) * groups for i in range(piece)]
+    starts = [sum(heights[:i]) for i in range(piece)]
+    b_rows = sum(heights)
     member, me = lax.axis_index("member"), lax.axis_index("lat")
     n_z = groups // 2
     z, core = me // 2, lax.rem(me, 2)
@@ -88,16 +92,24 @@
     def w_copy(b, slot):
         return pltpu.make_async_copy(w_hbm.at[pl.ds((n_blk - 1 - b) * blk_rows, blk_rows), :], stage.at[slot], w_sem.at[slot])
 
+    lane = me * lat_loc // LANES * LANES
+    pi_loc_in = pltpu.make_async_copy(
+        pi_hbm.at[pl.ds(top * piece * groups, piece * groups), pl.ds(top * l_step, l_step), pl.ds(pl.multiple_of(lane, LANES), LANES)],
+        pi_loc, in_sem.at[2])
+
     def start_loads():
         for s in range(n_slot):
             w_copy(s, s).start()
         for k in reversed(range(per_dev)):
             table_copy(pw_hbm, pw_v, pw_sem, k).start()
+            if k < top * piece:
+                table_copy(pi_hbm, pi_v, pi_sem, k).start()
             low, first = k * groups, (k // piece) * l_step
             if low > first:
                 pw_v[k, first:low, :] = jnp.zeros((low - first, n_lat), F32)
-                pi_v[k, first:low, :] = jnp.zeros((low - first, n_lat), F32)
-            table_copy(pi_hbm, pi_v, pi_sem, k).start()
+                if k < top * piece:
+                    pi_v[k, first:low, :] = jnp.zeros((low - first, n_lat), F32)
+        pi_loc_in.start()
         ti_in.start()
 
     tf_in.wait()
@@ -166,12 +178,65 @@
 
         lax.fori_loop(1, groups, done, 0)
 
+    n_hop = n_z // 2
+
+    def b_part(h, sgn):
+        if h < n_hop:
+            return pl.ds(0, b_rows)
+        return pl.ds(0 if sgn > 0 else b_rows // 2, b_rows // 2)
+
+    def chip(dz):
+        return lax.rem(z + dz + n_z, n_z)
+
+    def b_remote(s, part, to, sems, n):
+        return pltpu.make_async_remote_copy(
+            src_ref=b_all.at[s, part], dst_ref=b_all.at[s, part], send_sem=sems[0].at[n], recv_sem=sems[1].at[n],
+            device_id=(member, to), device_id_type=MESH)
+
+    def hop(h, sgn, arriving):
+        s = chip(-sgn * (h if arriving else h - 1)) * 2 + core
+        n = (h - 1) * 2 + (sgn < 0)
+        return b_remote(s, b_part(h, sgn), chip(sgn) * 2 + core, (hop_s, hop_r), n)
+
+    def sib(h, sgn, arriving):
+        s = chip(-sgn * h) * 2 + (1 - core if arriving else core)
+        n = 0 if h == 0 else (h - 1) * 2 + (sgn < 0) + 1
+        return b_remote(s, b_part(h, sgn), z * 2 + 1 - core, (sib_s, sib_r), n)
+
+    hops = [(h, sgn) for h in range(1, n_hop + 1) for sgn in (1, -1)]
+
+    def relay(h):
+        for sgn in (1, -1):
+            if h > 0:
+                hop(h, sgn, True).wait_recv()
+            if h < n_hop:
+                hop(h + 1, sgn, False).start()
+            if h > 0 or sgn > 0:
+                sib(h, sgn, False).start()
+
+    def b_done():
+        for h, sgn in hops:
+            hop(h, sgn, False).wait_send()
+        for h, sgn in [(0, 1)] + hops:
+            sib(h, sgn, False).wait_send()
+
     order = list(reversed(range(n_chunk)))
-    for j in order:
-        if j < n_chunk - 1:
-            lax.fori_loop(0, lat_loc // 2, lambda u, _, j=j: dft_out(j, u, f_b[u]) or 0, 0)
+
+    def send_fwd(j):
         own_copy(f_send, f_recv, j, j).start()
         send_all(fwd_copy, j)
+
+    def send_back(j):
+        own_copy(g_send, g_recv, j, n_chunk + j).start()
+        send_all(back_copy, j)
+        if j == 0:
+            send_all(back_copy, n_chunk)
+
+    send_fwd(top)
+    for j in order[1:]:
+        lax.fori_loop(0, lat_loc // 2, lambda u, _, j=j: dft_out(j, u, f_b[u]) or 0, 0)
+        if j == top - 1:
+            send_fwd(j)
 
     sign = jnp.where(lax.broadcasted_iota(jnp.int32, (rows, n_chan), 0) < piece, -1.0, 1.0).astype(F32)
 
@@ -225,6 +290,16 @@
             return 0
 
         lax.fori_loop(low // 8, l_max // 8, mix, 0)
+        if j == top:
+            for i in range(piece):
+                n_i = heights[i]
+                base = (l_max - n_i) * rows
+                re = coef[pl.ds(base + i, n_i, stride=rows), :]
+                im = coef[pl.ds(base + piece + i, n_i, stride=rows), :]
+                b_all[me, starts[i]:starts[i] + n_i, :] = jnp.concatenate([re, im], axis=1).astype(BF16)
+            relay(0)
+            send_fwd(top - 2)
+            continue
         for i in range(piece):
             k = j * piece + i
             table_copy(pi_hbm, pi_v, pi_sem, k).wait()
@@ -240,15 +315,37 @@
             return 0
 
         lax.fori_loop(0, groups, narrow, 0)
-        own_copy(g_send, g_recv, j, n_chunk + j).start()
-        send_all(back_copy, j)
+        relay(top - j)
+        if j == top - 1:
+            send_fwd(0)
+        if j == top - 2:
+            send_back(top - 1)
         if j == 0:
-            send_all(back_copy, n_chunk)
+            send_back(1)
+            send_back(0)
+
+    def own_rows(d, _):
+        for i in range(piece):
+            n_i = heights[i]
+            p_i = pltpu.roll(pi_loc[i * groups + d, l_step - n_i:, :], lax.rem(lane + LANES - me * lat_loc, LANES), 1)
+            g = dot(p_i.T[:lat_loc].astype(BF16), b_all[d, starts[i]:starts[i] + n_i, :], ((1,), (0,)))
+            wide[pl.ds(d * block + i, lat_loc, stride=rows), :] = g[:, :n_chan]
+            wide[pl.ds(d * block + piece + i, lat_loc, stride=rows), :] = g[:, n_chan:]
+        g_recv[top * groups + d] = wide[pl.ds(pl.multiple_of(d * block, block), block), :].astype(BF16)
+        return 0
 
     ti_in.wait()
-    for at, j in enumerate(order):
-        own_copy(g_send, g_recv, j, n_chunk + j).wait()
-        recv_all(back_copy, j)
+    back_order = [top - 1, top] + order[2:]
+    for at, j in enumerate(back_order):
+        if j == top:
+            relay(n_hop)
+            for h, sgn in [(0, 1)] + hops:
+                sib(h, sgn, True).wait_recv()
+            pi_loc_in.wait()
+            lax.fori_loop(0, groups, own_rows, 0)
+        else:
+            own_copy(g_send, g_recv, j, n_chunk + j).wait()
+            recv_all(back_copy, j)
         last = at == n_chunk - 1
 
         def inverse(u, _):
@@ -276,7 +373,9 @@
             lax.fori_loop(0, lat_loc // 2, inverse, 0)
     for j in order:
         sent_all(fwd_copy, j)
-        sent_all(back_copy, j)
+        if j < top:
+            sent_all(back_copy, j)
+    b_done()
     sent_all(back_copy, n_chunk)
 
 
@@ -289,6 +388,7 @@
         per_dev = l_max // groups
         rows = 2 * per_dev // N_CHUNK
         block = lat_loc * rows
+        b_rows = sum(l_max - k * groups for k in range(per_dev - per_dev // N_CHUNK, per_dev))
         fwd_tab, inv_tab = wave_tables(n_lon, groups, per_dev, N_CHUNK)
         w_rows = w_mix.transpose(0, 1, 3, 2).reshape(l_max * n_chan * 2, n_chan)
         hbm = pl.BlockSpec(memory_space=pltpu.HBM)
@@ -306,16 +406,19 @@
                 pltpu.VMEM((l_max * n_chan, 2 * n_chan), BF16),
                 pltpu.VMEM((4, 8 * n_chan * 2, n_chan), F32),
                 pltpu.VMEM((per_dev, l_max, n_lat), F32),
-                pltpu.VMEM((per_dev, l_max, n_lat), F32),
+                pltpu.VMEM((per_dev - per_dev // N_CHUNK, l_max, n_lat), F32),
                 exchange, exchange, exchange, exchange,
                 pltpu.VMEM((n_lat * rows, n_chan), F32),
                 pltpu.VMEM((l_max * rows, n_chan), F32),
+                pltpu.VMEM((groups, b_rows, 2 * n_chan), BF16),
+                pltpu.VMEM((l_max // N_CHUNK, l_max // N_CHUNK, LANES), F32),
                 pltpu.VMEM(fwd_tab.shape, BF16),
                 pltpu.VMEM(inv_tab.shape, BF16),
-                dma((2,)), dma((2, n_lon // LANES)), dma((per_dev,)), dma((per_dev,)), dma((4,)), dma((2 * N_CHUNK,)),
+                dma((3,)), dma((2, n_lon // LANES)), dma((per_dev,)), dma((per_dev,)), dma((4,)), dma((2 * N_CHUNK,)),
                 dma((N_CHUNK, groups)), dma((N_CHUNK, groups)), dma((N_CHUNK + 1, groups)), dma((N_CHUNK + 1, groups)),
+                dma((groups // 2,)), dma((groups // 2,)), dma((groups // 2 + 1,)), dma((groups // 2 + 1,)),
             ],
-            compiler_params=pltpu.CompilerParams(collective_id=0, has_side_effects=True, vmem_limit_bytes=54 * 2**20),
+            compiler_params=pltpu.CompilerParams(collective_id=0, has_side_effects=True, vmem_limit_bytes=56 * 2**20),
             name="spectral_layer",
         )(field_loc, p_fwd, p_inv, w_rows, fwd_tab, inv_tab)
         return jnp.concatenate([part.reshape(n_chan, lat_loc, LANES) for part in out], axis=2)

time: 113 us -> 109 us (0.965)
  Pallas kernels: 110 us -> 107 us
    pallas_call x1, Pallas kernels: 110 us -> 107 us  [local_layer(): pl.pallas_call(functools.partial(layer_kernel, (groups, n_chan, lat_loc,...]
where the time goes in v3:
time: 109 us
  Pallas kernels  107 us (98%)
  other arithmetic  2.29 us (2%)
    pallas_call x1, Pallas kernels, local_layer(): pl.pallas_call(functools.partial(layer_kernel, (groups, n_chan, lat_loc,...  107 us
    concatenate x1, other arithmetic, local_layer(): jnp.concatenate([part.reshape(n_chan, lat_loc, LANES) for part in out], a...  2.29 us

profile of v3, /device:TPU:21, one launch (start us, length us, event | category | flops | bytes accessed | tf_op | source)
XLA Modules:
  0.0 109.0 jit_solution(7678685466815105499)
XLA Ops:
  0.0 106.8 %spectral_layer.1 = (f32[2048,128]{1,0:T(8,128)S(1)}, f32[2048,128]{1,0:T(8,128)S(1)}, f32[2048,128]{1,0:T(8,128)S(1)}, f32[2048,128]{1,0:T(8,128)S(1)}) custom-call(f32[128,16,512]{2,1,0:T(8,128)} %f_hbm.1, f32[256,256,256]{2,1,0:T(8,128)} %pw_hbm.1, f32[256,256,256]{2,1,0:T(8,128)} %pi_hbm.1, f32[65536,128]{1,0:T(8,128)} %bitcast.11, ...), custom_call_target="tpu_custom_call" | custom-call | tf_op jit(solution)/shard_map/spectral_layer/pallas_call | solution.py:397
  106.8 2.3 %pad_maximum_fusion = f32[128,16,512]{2,1,0:T(8,128)} fusion(f32[128,16,128]{2,1,0:T(8,128)S(1)} %bitcast.10, f32[128,16,128]{2,1,0:T(8,128)S(1)} %bitcast.9, f32[128,16,128]{2,1,0:T(8,128)S(1)} %bitcast.8, f32[128,16,128]{2,1,0:T(8,128)S(1)} %bitcast.7), kind=kLoop, calls=%fused_computation | loop fusion | flops 3145728 | bytes 8388608 | tf_op jit(solution)/shard_map/concatenate | solution.py:424

commit v4 on v3

--- a/solution.py
+++ b/solution.py
@@ -14,6 +14,7 @@
 BF16 = jnp.bfloat16
 LANES = 128
 N_CHUNK = 4
+PAD = 8
 
 
 def wave_tables(n_lon, groups, per_dev, n_chunk):
@@ -34,7 +35,7 @@
 def layer_kernel(dims, f_hbm, pw_hbm, pi_hbm, w_hbm, tf_hbm, ti_hbm, *refs):
     n_out = dims[3] // LANES
     o_v, refs = refs[:n_out], refs[n_out:]
-    (f_v, f_b, h_v, w_v, stage, pw_v, pi_v, f_send, f_recv, g_send, g_recv, wide, coef, b_all, pi_loc, tf_v, ti_v,
+    (f_v, f_d, w_v, stage, pw_v, pi_v, f_send, f_recv, g_send, g_recv, wide, coef, b_all, pi_loc, tf_v, ti_v,
                  in_sem, f_sem, pw_sem, pi_sem, w_sem, own_sem, fs_sem, fr_sem, gs_sem, gr_sem, hop_s, hop_r, sib_s, sib_r) = refs
     groups, n_chan, lat_loc, n_lon, l_max, n_lat, n_chunk = dims
     per_dev = l_max // groups
@@ -113,7 +114,8 @@
         ti_in.start()
 
     tf_in.wait()
-    f_rows = f_v.reshape(n_col, n_chan * lat_loc, LANES)
+    tall = lat_loc + PAD
+    f_rows = f_v.reshape(n_col, n_chan * tall, LANES)
 
     def dft_out(j, u, f_pair):
         r = dot(tf_v[j * groups * rows:(j + 1) * groups * rows, :], f_pair, ((1,), (1,)))
@@ -124,25 +126,25 @@
     def dft_first(u, _):
         pair = []
         for e in range(2):
-            here = pl.ds(2 * u + e, n_chan, stride=lat_loc)
-            pair.append(jnp.concatenate([f_rows[x, here, :] for x in range(n_col)], axis=1))
-        f_pair = jnp.concatenate(pair, axis=0).astype(BF16)
-        f_b[u] = f_pair
-        dft_out(n_chunk - 1, u, f_pair)
+            here = pl.ds(2 * u + e, n_chan, stride=tall)
+            f_t = jnp.concatenate([f_rows[x, here, :] for x in range(n_col)], axis=1)
+            f_d[2 * u + e] = f_t
+            pair.append(f_t.astype(BF16))
+        dft_out(top, u, jnp.concatenate(pair, axis=0))
         return 0
 
-    for h in range(2):
-        for x in range(n_col):
-            f_in(h, x).wait()
-        if h == 1:
-            start_loads()
-        lax.fori_loop(h * half // 2, (h + 1) * half // 2, dft_first, 0)
-    pl.semaphore_wait(barrier, groups - 1)
-
-    def fwd_copy(j, to, slot):
+    def dft_next(j, u, _):
+        f_pair = jnp.concatenate([f_d[2 * u + e].astype(BF16) for e in range(2)], axis=0)
+        dft_out(j, u, f_pair)
+        return 0
+
+    def fwd_copy(p, to, slot):
+        j, part = (p, pl.ds(0, block)) if p < top else (top, pl.ds(0, block // 2))
+        if p == n_chunk:
+            part = pl.ds(block // 2, block // 2)
         return pltpu.make_async_remote_copy(
-            src_ref=f_send.at[j * groups + to], dst_ref=f_recv.at[j * groups + slot], send_sem=fs_sem.at[j, to],
-            recv_sem=fr_sem.at[j, slot], device_id=(member, to), device_id_type=MESH)
+            src_ref=f_send.at[j * groups + to, part], dst_ref=f_recv.at[j * groups + slot, part], send_sem=fs_sem.at[p, to],
+            recv_sem=fr_sem.at[p, slot], device_id=(member, to), device_id_type=MESH)
 
     def back_copy(p, to, slot):
         j, part = (p, pl.ds(0, block)) if p else (0, pl.ds(0, block // 2))
@@ -232,9 +234,19 @@
         if j == 0:
             send_all(back_copy, n_chunk)
 
-    send_fwd(top)
+    for h in range(2):
+        for x in range(n_col):
+            f_in(h, x).wait()
+        if h == 1:
+            start_loads()
+        lax.fori_loop(h * half // 2, (h + 1) * half // 2, dft_first, 0, unroll=2)
+        if h == 0:
+            pl.semaphore_wait(barrier, groups - 1)
+            send_all(fwd_copy, top)
+    own_copy(f_send, f_recv, top, top).start()
+    send_all(fwd_copy, n_chunk)
     for j in order[1:]:
-        lax.fori_loop(0, lat_loc // 2, lambda u, _, j=j: dft_out(j, u, f_b[u]) or 0, 0)
+        lax.fori_loop(0, lat_loc // 2, functools.partial(dft_next, j), 0, unroll=2)
         if j == top - 1:
             send_fwd(j)
 
@@ -262,6 +274,8 @@
         lax.fori_loop(at * blk_chunk, (at + 1) * blk_chunk, load_w, 0)
         own_copy(f_send, f_recv, j, j).wait()
         recv_all(fwd_copy, j)
+        if j == top:
+            recv_all(fwd_copy, n_chunk)
         low = j * l_step
         n_l = l_max - low
 
@@ -354,15 +368,16 @@
                 t = 2 * u + half
                 g_t = pair[:, half * rows:(half + 1) * rows, :].reshape(groups * rows, n_chan)
                 h = dot(g_t.T.astype(BF16), ti_v[j * groups * rows:(j + 1) * groups * rows, :], ((1,), (0,)))
-                if at > 0:
-                    h = h + h_v[t]
-                if last:
-                    here = pl.ds(t, n_chan, stride=lat_loc)
-                    g = jax.nn.gelu(h)
-                    for x in range(n_col):
-                        o_v[x][here, :] = f_rows[x, here, :] + g[:, x * LANES:(x + 1) * LANES]
-                else:
-                    h_v[t] = h
+                kept = pl.ds(pl.multiple_of(t * n_chan, n_chan), n_chan)
+                for x in range(n_col):
+                    lanes = slice(x * LANES, (x + 1) * LANES)
+                    h_x = h[:, lanes]
+                    if at > 0:
+                        h_x = h_x + f_rows[x, kept, :]
+                    if last:
+                        o_v[x][pl.ds(t, n_chan, stride=tall), :] = f_d[t, :, lanes] + jax.nn.gelu(h_x)
+                    else:
+                        f_rows[x, kept, :] = h_x
             return 0
 
         if last:
@@ -376,6 +391,7 @@
         if j < top:
             sent_all(back_copy, j)
     b_done()
+    sent_all(fwd_copy, n_chunk)
     sent_all(back_copy, n_chunk)
 
 
@@ -396,12 +412,11 @@
         dma = pltpu.SemaphoreType.DMA
         out = pl.pallas_call(
             functools.partial(layer_kernel, (groups, n_chan, lat_loc, n_lon, l_max, n_lat, N_CHUNK)),
-            out_shape=[pltpu.VMEM((n_chan * lat_loc, LANES), F32)] * (n_lon // LANES),
+            out_shape=[pltpu.VMEM((n_chan * (lat_loc + PAD), LANES), F32)] * (n_lon // LANES),
             in_specs=[hbm] * 6,
             out_specs=[pl.BlockSpec(memory_space=pltpu.VMEM)] * (n_lon // LANES),
             scratch_shapes=[
-                pltpu.VMEM((n_lon // LANES, n_chan, lat_loc, LANES), F32),
-                pltpu.VMEM((lat_loc // 2, 2 * n_chan, n_lon), BF16),
+                pltpu.VMEM((n_lon // LANES, n_chan, lat_loc + PAD, LANES), F32),
                 pltpu.VMEM((lat_loc, n_chan, n_lon), F32),
                 pltpu.VMEM((l_max * n_chan, 2 * n_chan), BF16),
                 pltpu.VMEM((4, 8 * n_chan * 2, n_chan), F32),
@@ -415,12 +430,12 @@
                 pltpu.VMEM(fwd_tab.shape, BF16),
                 pltpu.VMEM(inv_tab.shape, BF16),
                 dma((3,)), dma((2, n_lon // LANES)), dma((per_dev,)), dma((per_dev,)), dma((4,)), dma((2 * N_CHUNK,)),
-                dma((N_CHUNK, groups)), dma((N_CHUNK, groups)), dma((N_CHUNK + 1, groups)), dma((N_CHUNK + 1, groups)),
+                dma((N_CHUNK + 1, groups)), dma((N_CHUNK + 1, groups)), dma((N_CHUNK + 1, groups)), dma((N_CHUNK + 1, groups)),
                 dma((groups // 2,)), dma((groups // 2,)), dma((groups // 2 + 1,)), dma((groups // 2 + 1,)),
             ],
             compiler_params=pltpu.CompilerParams(collective_id=0, has_side_effects=True, vmem_limit_bytes=56 * 2**20),
             name="spectral_layer",
         )(field_loc, p_fwd, p_inv, w_rows, fwd_tab, inv_tab)
-        return jnp.concatenate([part.reshape(n_chan, lat_loc, LANES) for part in out], axis=2)
+        return jnp.concatenate([part.reshape(n_chan, lat_loc + PAD, LANES)[:, :lat_loc] for part in out], axis=2)
 
     return jax.shard_map(local_layer, mesh=mesh, in_specs=(P("member", "lat", None), P(), P(), P()), out_specs=P("member", "lat", None), check_vma=False)

time: 109 us -> 107 us (0.982)
  Pallas kernels: 107 us -> 104 us
    pallas_call x1, Pallas kernels: 107 us -> 104 us  [local_layer(): pl.pallas_call(functools.partial(layer_kernel, (groups, n_chan, lat_loc,...]
where the time goes in v4:
time: 107 us
  Pallas kernels  104 us (97%)
  other arithmetic  2.29 us (2%)
    pallas_call x1, Pallas kernels, local_layer(): pl.pallas_call(functools.partial(layer_kernel, (groups, n_chan, lat_loc,...  104 us
    concatenate x1, other arithmetic, local_layer(): jnp.concatenate([part.reshape(n_chan, lat_loc + PAD, LANES)[:, :lat_loc]...  2.29 us

profile of v4, /device:TPU:21, one launch (start us, length us, event | category | flops | bytes accessed | tf_op | source)
XLA Modules:
  0.0 106.7 jit_solution(11053801761726863936)
XLA Ops:
  0.0 104.1 %spectral_layer.1 = (f32[3072,128]{1,0:T(8,128)S(1)}, f32[3072,128]{1,0:T(8,128)S(1)}, f32[3072,128]{1,0:T(8,128)S(1)}, f32[3072,128]{1,0:T(8,128)S(1)}) custom-call(f32[128,16,512]{2,1,0:T(8,128)} %f_hbm.1, f32[256,256,256]{2,1,0:T(8,128)} %pw_hbm.1, f32[256,256,256]{2,1,0:T(8,128)} %pi_hbm.1, f32[65536,128]{1,0:T(8,128)} %bitcast.11, ...), custom_call_target="tpu_custom_call" | custom-call | tf_op jit(solution)/shard_map/spectral_layer/pallas_call | solution.py:413
  104.1 0.1 slice.16
  104.2 0.1 slice.17
  104.3 0.1 slice.18
  104.4 0.1 slice.19
  104.4 2.3 %pad_maximum_fusion = f32[128,16,512]{2,1,0:T(8,128)} fusion(f32[128,16,128]{2,1,0:T(8,128)S(1)} %slice.19, f32[128,16,128]{2,1,0:T(8,128)S(1)} %slice.18, f32[128,16,128]{2,1,0:T(8,128)S(1)} %slice.17, f32[128,16,128]{2,1,0:T(8,128)S(1)} %slice.16), kind=kLoop, calls=%fused_computation | loop fusion | flops 3145728 | bytes 8388608 | tf_op jit(solution)/shard_map/concatenate | solution.py:439

commit v5 on v4

--- a/solution.py
+++ b/solution.py
@@ -42,6 +42,7 @@
     piece = per_dev // n_chunk
     rows = 2 * piece
     block = lat_loc * rows
+    n_first = block * 3 // 4
     l_step = l_max // n_chunk
     top = n_chunk - 1
     heights = [l_max - (top * piece + i) * groups for i in range(piece)]
@@ -147,9 +148,9 @@
             recv_sem=fr_sem.at[p, slot], device_id=(member, to), device_id_type=MESH)
 
     def back_copy(p, to, slot):
-        j, part = (p, pl.ds(0, block)) if p else (0, pl.ds(0, block // 2))
+        j, part = (p, pl.ds(0, block)) if p else (0, pl.ds(0, n_first))
         if p == n_chunk:
-            j, part = 0, pl.ds(block // 2, block // 2)
+            j, part = 0, pl.ds(n_first, block - n_first)
         return pltpu.make_async_remote_copy(
             src_ref=g_send.at[j * groups + to, part], dst_ref=g_recv.at[j * groups + slot, part], send_sem=gs_sem.at[p, to],
             recv_sem=gr_sem.at[p, slot], device_id=(member, to), device_id_type=MESH)
@@ -381,9 +382,10 @@
             return 0
 
         if last:
-            lax.fori_loop(0, lat_loc // 4, inverse, 0)
+            first = n_first // rows // 2
+            lax.fori_loop(0, first, inverse, 0, unroll=2)
             recv_all(back_copy, n_chunk)
-            lax.fori_loop(lat_loc // 4, lat_loc // 2, inverse, 0)
+            lax.fori_loop(first, lat_loc // 2, inverse, 0, unroll=2)
         else:
             lax.fori_loop(0, lat_loc // 2, inverse, 0)
     for j in order:
@@ -393,6 +395,18 @@
     b_done()
     sent_all(fwd_copy, n_chunk)
     sent_all(back_copy, n_chunk)
+
+
+def out_kernel(n_chan, lat_loc, *refs):
+    parts, o_hbm, sem = refs[:-2], refs[-2], refs[-1]
+    copies = []
+    for x, part in enumerate(parts):
+        rows = part.reshape(n_chan, part.shape[0] // n_chan, LANES).at[:, pl.ds(0, lat_loc), :]
+        copies.append(pltpu.make_async_copy(rows, o_hbm.at[:, :, pl.ds(x * LANES, LANES)], sem.at[x]))
+    for copy in copies:
+        copy.start()
+    for copy in copies:
+        copy.wait()
 
 
 def solution(mesh):
@@ -436,6 +450,15 @@
             compiler_params=pltpu.CompilerParams(collective_id=0, has_side_effects=True, vmem_limit_bytes=56 * 2**20),
             name="spectral_layer",
         )(field_loc, p_fwd, p_inv, w_rows, fwd_tab, inv_tab)
-        return jnp.concatenate([part.reshape(n_chan, lat_loc + PAD, LANES)[:, :lat_loc] for part in out], axis=2)
+        vmem = pl.BlockSpec(memory_space=pltpu.VMEM)
+        return pl.pallas_call(
+            functools.partial(out_kernel, n_chan, lat_loc),
+            out_shape=jax.ShapeDtypeStruct(field_loc.shape, F32),
+            in_specs=[vmem] * len(out),
+            out_specs=hbm,
+            scratch_shapes=[dma((len(out),))],
+            compiler_params=pltpu.CompilerParams(vmem_limit_bytes=2**20),
+            name="result_out",
+        )(*out)
 
     return jax.shard_map(local_layer, mesh=mesh, in_specs=(P("member", "lat", None), P(), P(), P()), out_specs=P("member", "lat", None), check_vma=False)

time: 107 us -> 106 us (level)
  other arithmetic: 2.29 us -> 0 us
  Pallas kernels: 104 us -> 106 us
    concatenate x1 -> x0, other arithmetic: 2.29 us -> none  [local_layer(): jnp.concatenate([part.reshape(n_chan, lat_loc + PAD, LANES)[:, :lat_loc]...]
    pallas_call x0 -> x1, Pallas kernels: none -> 2.04 us  [local_layer(): pl.pallas_call(functools.partial(out_kernel, n_chan, lat_loc), out_shape=...]
where the time goes in v5:
time: 106 us
  Pallas kernels  106 us (100%)
    pallas_call x1, Pallas kernels, local_layer(): pl.pallas_call(functools.partial(layer_kernel, (groups, n_chan, lat_loc,...  103 us

profile of v5, /device:TPU:21, one launch (start us, length us, event | category | flops | bytes accessed | tf_op | source)
XLA Modules:
  0.0 105.5 jit_solution(12608682909562772631)
XLA Ops:
  0.0 103.5 %spectral_layer.1 = (f32[3072,128]{1,0:T(8,128)S(1)}, f32[3072,128]{1,0:T(8,128)S(1)}, f32[3072,128]{1,0:T(8,128)S(1)}, f32[3072,128]{1,0:T(8,128)S(1)}) custom-call(f32[128,16,512]{2,1,0:T(8,128)} %f_hbm.1, f32[256,256,256]{2,1,0:T(8,128)} %pw_hbm.1, f32[256,256,256]{2,1,0:T(8,128)} %pi_hbm.1, f32[65536,128]{1,0:T(8,128)} %bitcast.3, ...), custom_call_target="tpu_custom_call" | custom-call | tf_op jit(solution)/shard_map/spectral_layer/pallas_call | solution.py:427
  103.5 2.0 %result_out.1 = f32[128,16,512]{2,1,0:T(8,128)} custom-call(f32[3072,128]{1,0:T(8,128)S(1)} %get-tuple-element.9.refs_0_, f32[3072,128]{1,0:T(8,128)S(1)} %get-tuple-element.10.refs_1_, f32[3072,128]{1,0:T(8,128)S(1)} %get-tuple-element.11.refs_2_, f32[3072,128]{1,0:T(8,128)S(1)} %get-tuple-element.12.refs_3_), custom_call_target="tpu_custom_call" | custom-call | tf_op jit(solution)/shard_map/result_out/pallas_call | solution.py:454

commit v6 on v5

--- a/solution.py
+++ b/solution.py
@@ -75,12 +75,16 @@
         part = pl.ds(h * half, half)
         return pltpu.make_async_copy(f_hbm.at[:, part, pl.ds(x * LANES, LANES)], f_v.at[x, :, part, :], f_sem.at[h, x])
 
-    tf_in = pltpu.make_async_copy(tf_hbm, tf_v, in_sem.at[0])
+    n_top = groups * rows
+    n_low = tf_hbm.shape[0] - n_top
+    tf_in = pltpu.make_async_copy(tf_hbm.at[pl.ds(n_low, n_top)], tf_v.at[pl.ds(n_low, n_top)], in_sem.at[0])
+    tf_rest = pltpu.make_async_copy(tf_hbm.at[pl.ds(0, n_low)], tf_v.at[pl.ds(0, n_low)], in_sem.at[3])
     ti_in = pltpu.make_async_copy(ti_hbm, ti_v, in_sem.at[1])
     tf_in.start()
     for h in range(2):
         for x in range(n_col):
             f_in(h, x).start()
+    tf_rest.start()
 
     def table_copy(src, dst, sem, k):
         low = k * groups
@@ -240,12 +244,13 @@
             f_in(h, x).wait()
         if h == 1:
             start_loads()
-        lax.fori_loop(h * half // 2, (h + 1) * half // 2, dft_first, 0, unroll=2)
+        lax.fori_loop(h * half // 2, (h + 1) * half // 2, dft_first, 0, unroll=4)
         if h == 0:
             pl.semaphore_wait(barrier, groups - 1)
             send_all(fwd_copy, top)
     own_copy(f_send, f_recv, top, top).start()
     send_all(fwd_copy, n_chunk)
+    tf_rest.wait()
     for j in order[1:]:
         lax.fori_loop(0, lat_loc // 2, functools.partial(dft_next, j), 0, unroll=2)
         if j == top - 1:
@@ -443,7 +448,7 @@
                 pltpu.VMEM((l_max // N_CHUNK, l_max // N_CHUNK, LANES), F32),
                 pltpu.VMEM(fwd_tab.shape, BF16),
                 pltpu.VMEM(inv_tab.shape, BF16),
-                dma((3,)), dma((2, n_lon // LANES)), dma((per_dev,)), dma((per_dev,)), dma((4,)), dma((2 * N_CHUNK,)),
+                dma((4,)), dma((2, n_lon // LANES)), dma((per_dev,)), dma((per_dev,)), dma((4,)), dma((2 * N_CHUNK,)),
                 dma((N_CHUNK + 1, groups)), dma((N_CHUNK + 1, groups)), dma((N_CHUNK + 1, groups)), dma((N_CHUNK + 1, groups)),
                 dma((groups // 2,)), dma((groups // 2,)), dma((groups // 2 + 1,)), dma((groups // 2 + 1,)),
             ],

time: 106 us -> 105 us (level)
  no operation moved by 1% of the time
where the time goes in v6:
time: 105 us
  Pallas kernels  105 us (100%)
    pallas_call x1, Pallas kernels, local_layer(): pl.pallas_call(functools.partial(layer_kernel, (groups, n_chan, lat_loc,...  103 us

profile of v6, /device:TPU:21, one launch (start us, length us, event | category | flops | bytes accessed | tf_op | source)
XLA Modules:
  0.0 105.4 jit_solution(16462546951276211816)
XLA Ops:
  0.0 103.3 %spectral_layer.1 = (f32[3072,128]{1,0:T(8,128)S(1)}, f32[3072,128]{1,0:T(8,128)S(1)}, f32[3072,128]{1,0:T(8,128)S(1)}, f32[3072,128]{1,0:T(8,128)S(1)}) custom-call(f32[128,16,512]{2,1,0:T(8,128)} %f_hbm.1, f32[256,256,256]{2,1,0:T(8,128)} %pw_hbm.1, f32[256,256,256]{2,1,0:T(8,128)} %pi_hbm.1, f32[65536,128]{1,0:T(8,128)} %bitcast.3, ...), custom_call_target="tpu_custom_call" | custom-call | tf_op jit(solution)/shard_map/spectral_layer/pallas_call | solution.py:432
  103.3 2.0 %result_out.1 = f32[128,16,512]{2,1,0:T(8,128)} custom-call(f32[3072,128]{1,0:T(8,128)S(1)} %get-tuple-element.9.refs_0_, f32[3072,128]{1,0:T(8,128)S(1)} %get-tuple-element.10.refs_1_, f32[3072,128]{1,0:T(8,128)S(1)} %get-tuple-element.11.refs_2_, f32[3072,128]{1,0:T(8,128)S(1)} %get-tuple-element.12.refs_3_), custom_call_target="tpu_custom_call" | custom-call | tf_op jit(solution)/shard_map/result_out/pallas_call | solution.py:459
